TPU v7x, 32 devices: a whole 2x2x4 slice. The times are simulated.
32 devices in a mesh: rep: 4 (over x, y), pp: 8 (over z, core).
Axes of the slice: x: 2, y: 2, z: 4, core: 2. Of those that a mesh axis runs over, the one named last changes fastest.
Arguments:
- x: bfloat16 [64, 512, 640], P('rep'), parts along dimension 0
- dy: bfloat16 [64, 512, 640], P('rep'), parts along dimension 0
- w_gate: bfloat16 [8, 640, 1536], P('pp')
- w_up: bfloat16 [8, 640, 1536], P('pp')
- w_down: bfloat16 [8, 1536, 640], P('pp')
Outputs:
- output 1: bfloat16 [32, 640, 1536], P(('rep', 'pp')), parts along dimension 0
- output 2: bfloat16 [32, 640, 1536], P(('rep', 'pp')), parts along dimension 0
- output 3: bfloat16 [32, 1536, 640], P(('rep', 'pp')), parts along dimension 0
There are 4 independent parts. A program takes and returns all parts, laid end to end along the dimension named above; an argument that names none is the same for every part.
All inputs are finite; a program needn't handle non-finite values.
Results may differ from a plain program's by a relative error of at most 0.0253.
Values are sent between devices in bfloat16 or wider.
A program may use at most 2 GiB of HBM per device.

v0:
```python
import jax
import jax.numpy as jnp
from jax import lax
from jax.sharding import PartitionSpec as P

NAMES = ("w_gate", "w_up", "w_down")


def matmul(a, w):
    return jnp.dot(a, w, preferred_element_type=jnp.float32).astype(jnp.bfloat16)


def normed(h):
    wide = h.astype(jnp.float32)
    scale = lax.rsqrt(jnp.mean(wide**2, -1, keepdims=True) + 1e-6)
    return (wide * scale).astype(jnp.bfloat16)


def layer(h, w):
    a = normed(h)
    gate = jnp.dot(a, w["w_gate"], preferred_element_type=jnp.float32)
    up = jnp.dot(a, w["w_up"], preferred_element_type=jnp.float32)
    return h + matmul((jax.nn.silu(gate) * up).astype(jnp.bfloat16), w["w_down"])


def stage(weights, h):
    for number in range(weights["w_gate"].shape[0]):
        h = layer(h, {name: w[number] for name, w in weights.items()})
    return h


def solution(mesh):
    stages = mesh.shape["pp"]
    onward = [(i, i + 1) for i in range(stages - 1)]
    back_again = [(i + 1, i) for i in range(stages - 1)]

    def step(x, dy, *arrays):
        weights = dict(zip(NAMES, arrays, strict=True))
        micro, me = x.shape[0], lax.axis_index("pp")
        kept, came = jnp.zeros_like(x), jnp.zeros_like(x[0])
        for t in range(micro + stages - 1):
            number = jnp.clip(t - me, 0, micro - 1)
            at_work = (t >= me) & (t - me < micro)
            h = jnp.where(me == 0, x[min(t, micro - 1)], came)
            was = lax.dynamic_index_in_dim(kept, number, 0, keepdims=False)
            kept = lax.dynamic_update_index_in_dim(kept, jnp.where(at_work, h, was), number, 0)
            came = lax.ppermute(stage(weights, h), "pp", onward)
        total = {name: jnp.zeros(w.shape, jnp.float32) for name, w in weights.items()}
        came, behind = jnp.zeros_like(x[0]), stages - 1 - me
        for t in range(micro + stages - 1):
            number = jnp.clip(t - behind, 0, micro - 1)
            at_work = (t >= behind) & (t - behind < micro)
            by_y = jnp.where(behind == 0, dy[min(t, micro - 1)], came)
            _, back = jax.vjp(stage, weights, lax.dynamic_index_in_dim(kept, number, 0, keepdims=False))
            by_w, by_h = back(by_y)
            total = {name: total[name] + jnp.where(at_work, by_w[name].astype(jnp.float32), 0.0) for name in NAMES}
            came = lax.ppermute(by_h, "pp", back_again)
        return tuple(total[name].astype(jnp.bfloat16) for name in NAMES)

    return jax.shard_map(
        step,
        mesh=mesh,
        in_specs=(P("rep", None, None),) * 2 + (P("pp", None, None),) * 3,
        out_specs=(P(("rep", "pp"), None, None),) * 3,
        check_vma=False,
    )
```

profile of v0, /device:TPU:3, one launch (start us, length us, event | category | flops | bytes accessed | tf_op | source)
XLA Modules:
  0.0 1226.1 jit_solution(6538709881105234572)
XLA Ops:
  16.4 7.5 collective-permute-done
  38.6 7.5 collective-permute-done.1
  61.0 7.3 collective-permute-done.2
  83.8 7.5 collective-permute-done.3
  106.9 7.5 collective-permute-done.4
  131.5 7.1 collective-permute-done.5
  143.9 6.9 fusion.923
  155.2 7.5 collective-permute-done.6
  179.4 7.5 collective-permute-done.7
  203.7 7.3 collective-permute-done.8
  227.7 7.5 collective-permute-done.9
  240.5 6.9 fusion.911
  359.9 7.0 fusion.896
  384.3 7.0 fusion.893
  408.7 7.0 fusion.890
  479.4 7.0 fusion.881
  690.1 7.0 collective-permute-done.25
  739.6 7.0 collective-permute-done.27
  764.8 7.0 collective-permute-done.28
  815.1 7.0 collective-permute-done.30
  840.2 7.0 collective-permute-done.31
  890.4 7.1 collective-permute-done.33
  915.7 7.0 collective-permute-done.34
  965.8 7.1 collective-permute-done.36
  991.1 7.0 collective-permute-done.37
  1041.2 7.1 collective-permute-done.39
  1066.4 6.9 collective-permute-done.40
  1116.5 7.1 collective-permute-done.42
  1148.1 7.0 collective-permute-done.43
  1157.8 21.6 %fusion.94 = bf16[1,640,1536]{2,1,0:T(8,128)(2,1)} fusion(bf16[512,1536]{1,0:T(8,128)(2,1)} %convolution_convert_fusion.69, bf16[640,1536]{1,0:T(8,128)(2,1)} %convolution_convert_fusion.1, bf16[640,1536]{1,0:T(8,128)(2,1)} %convolution_convert_fusion.2, bf16[640,1536]{1,0:T(8,128)(2,1)} %convolution_convert_fusion.3, ...), kind=kOutput, calls=%fused_computation.325 | convolution fusion | flops 1081147392 | bytes 50595868 | tf_op jit(solution)/shard_map/transpose(jvp())/dot_general | solution.py:22
  1179.4 23.4 %fusion.96 = bf16[1,640,1536]{2,1,0:T(8,128)(2,1)} fusion(f32[512,1536]{1,0:T(8,128)} %fusion.278, f32[512,1536]{1,0:T(8,128)} %fusion.188, bf16[512,1536]{1,0:T(8,128)(2,1)} %convolution_convert_fusion.69, bf16[640,1536]{1,0:T(8,128)(2,1)} %convolution_convert_fusion.24, bf16[640,1536]{1,0:T(8,128)(2,1)} %convolution_convert_fusion.25, ...), kind=kOutput, calls=%fused_computation.327 | convolution fusion | flops 1085079552 | bytes 53741596 | tf_op jit(solution)/shard_map/transpose(jvp())/dot_general | solution.py:21
  1202.8 22.7 %fusion.95 = bf16[1,1536,640]{2,1,0:T(8,128)(2,1)} fusion(bf16[1536,640]{1,0:T(8,128)(2,1)} %convolution_convert_fusion.47, bf16[1536,640]{1,0:T(8,128)(2,1)} %convolution_convert_fusion.48, bf16[1536,640]{1,0:T(8,128)(2,1)} %convolution_convert_fusion.49, bf16[1536,640]{1,0:T(8,128)(2,1)} %convolution_convert_fusion.50, ...), kind=kOutput, calls=%fused_computation.326 | convolution fusion | flops 1080492032 | bytes 52822040 | tf_op jit(solution)/shard_map/transpose(jvp())/dot_general | solution.py:10
  (731 shorter events, 946.9 us)
Async XLA Ops:
  34.2 11.9 collective-permute-start.1
  126.6 11.9 collective-permute-start.5
  223.3 11.9 collective-permute-start.9
  247.4 12.1 collective-permute-start.10
  296.1 12.0 collective-permute-start.12
  319.2 12.0 collective-permute-start.13
  342.5 12.0 collective-permute-start.14
  366.9 12.0 collective-permute-start.15
  391.3 12.0 collective-permute-start.16
  415.6 12.0 collective-permute-start.17
  438.8 12.0 collective-permute-start.18
  462.0 12.0 collective-permute-start.19
  486.4 11.9 collective-permute-start.20
  549.8 55.1 %collective-permute-start.22 = (bf16[512,640]{1,0:T(8,128)(2,1)S(1)}, bf16[512,640]{1,0:T(8,128)(2,1)S(1)}, u32[]{:S(2)}, u32[]{:S(2)}) collective-permute-start(bf16[512,640]{1,0:T(8,128)(2,1)S(1)} %fusion.1099), channel_id=1, source_target_pairs={{1,0},{2,1},{3,2},{4,3},{5,4},{6,5},{7,6},{9,8},{10,9},{11,10},{12... | collective-permute-start | bytes 1966088 | tf_op jit(solution)/shard_map/ppermute | solution.py:57
  618.5 14.5 %collective-permute-start.23 = (bf16[512,640]{1,0:T(8,128)(2,1)S(1)}, bf16[512,640]{1,0:T(8,128)(2,1)S(1)}, u32[]{:S(2)}, u32[]{:S(2)}) collective-permute-start(bf16[512,640]{1,0:T(8,128)(2,1)S(1)} %fusion.1098), channel_id=1, source_target_pairs={{1,0},{2,1},{3,2},{4,3},{5,4},{6,5},{7,6},{9,8},{10,9},{11,10},{12... | collective-permute-start | bytes 1966088 | tf_op jit(solution)/shard_map/ppermute | solution.py:57
  654.1 12.7 %collective-permute-start.24 = (bf16[512,640]{1,0:T(8,128)(2,1)S(1)}, bf16[512,640]{1,0:T(8,128)(2,1)S(1)}, u32[]{:S(2)}, u32[]{:S(2)}) collective-permute-start(bf16[512,640]{1,0:T(8,128)(2,1)S(1)} %fusion.1097), channel_id=1, source_target_pairs={{1,0},{2,1},{3,2},{4,3},{5,4},{6,5},{7,6},{9,8},{10,9},{11,10},{12... | collective-permute-start | bytes 1966088 | tf_op jit(solution)/shard_map/ppermute | solution.py:57
  685.1 11.9 collective-permute-start.25
  734.7 11.9 collective-permute-start.27
  759.9 11.9 collective-permute-start.28
  785.1 11.9 collective-permute-start.29
  810.2 11.9 collective-permute-start.30
  835.4 11.9 collective-permute-start.31
  860.4 11.9 collective-permute-start.32
  885.5 11.9 collective-permute-start.33
  910.8 11.9 collective-permute-start.34
  935.8 11.9 collective-permute-start.35
  961.0 11.9 collective-permute-start.36
  1011.2 11.9 collective-permute-start.38
  1036.3 11.9 collective-permute-start.39
  1061.4 11.9 collective-permute-start.40
  1086.5 11.9 collective-permute-start.41
  1111.6 11.9 collective-permute-start.42
  (146 other events, 1063.7 us)
where the time goes:
time: 1240 us; the launch traced here: 1230 us
  matrix products  714 us (58%)
  waiting for transfers between devices  225 us (18%)
  starting transfers between devices  147 us (12%)
  other arithmetic  79.8 us (6%)
  local copies, waits for them, and re-layouts  56.7 us (5%)
    dot_general x68, matrix products, matmul(): jnp.dot(a, w, preferred_element_type=jnp.float32).astype(jnp.bfloat16)  276 us
    dot_general x90, matrix products, layer(): gate = jnp.dot(a, w['w_gate'], preferred_element_type=jnp.float32)  241 us
    dot_general x68, matrix products, layer(): up = jnp.dot(a, w['w_up'], preferred_element_type=jnp.float32)  197 us
    ppermute x22, waiting for transfers between devices, step(): came = lax.ppermute(by_h, 'pp', back_again)  138 us
    ppermute x22, starting transfers between devices, step(): came = lax.ppermute(stage(weights, h), 'pp', onward)  99.4 us
    ppermute x22, waiting for transfers between devices, step(): came = lax.ppermute(stage(weights, h), 'pp', onward)  86.1 us
    ppermute x22, starting transfers between devices, step(): came = lax.ppermute(by_h, 'pp', back_again)  47.6 us
    dynamic_update_slice x23, other arithmetic, step(): lax.dynamic_update_index_in_dim(kept, jnp.where(at_work, h, was), number, 0)  35.6 us
  transfers between devices with their start and end apart: 44, of which 40 were waited for; matrix products, arithmetic and copies ran while one was open for 16% of the time, Pallas kernels for 0%

commit v1 on v0

v1 whole, which is shorter than its diff:
```python
import functools

import jax
import jax.numpy as jnp
from jax import lax
from jax.experimental import pallas as pl
from jax.experimental.pallas import tpu as pltpu
from jax.sharding import PartitionSpec as P

f32, bf16 = jnp.float32, jnp.bfloat16
MESH = pl.DeviceIdType.MESH
CHUNK = 256


def dot(a, b):
    return lax.dot_general(a, b, (((1,), (0,)), ((), ())), preferred_element_type=f32)


def dot_t(a, b):
    return lax.dot_general(a, b, (((1,), (1,)), ((), ())), preferred_element_type=f32)


def rounded(v):
    return v.astype(bf16).astype(f32)


def tiles(total, size):
    return [pl.ds(i, size) for i in range(0, total, size)]


def inverse_rms(h):
    return lax.rsqrt(jnp.mean(h * h, 0, keepdims=True) + 1e-6)


def transpose_into(dst, src, rows, cols):
    for r in tiles(rows, 128):
        for c in tiles(cols, 128):
            dst[c, r] = src[r, c].T


def f_norm(h, a, out):
    wide = h[...].astype(f32)
    a[...] = (wide * inverse_rms(wide)).astype(bf16)
    out[...] = h[...]


def f_up(w_gate, w_up, a, s_out, t_out, mid):
    for r in tiles(mid.shape[0], 256):
        g = dot(w_gate[r, :], a[...])
        u = dot(w_up[r, :], a[...])
        sig = 1.0 / (1.0 + jnp.exp(-g))
        s = g * sig
        s_out[r, :] = s
        t_out[r, :] = u * (sig + s * (1.0 - sig))
        mid[r, :] = (s * u).astype(bf16)


def f_down(w_down, mid, out):
    for r in tiles(out.shape[0], 320):
        o = rounded(dot(w_down[r, :], mid[...]))
        out[r, :] = (out[r, :].astype(f32) + o).astype(bf16)


def b_mid(w_down, dy, s_in, t_in, dg, du):
    for r in tiles(dg.shape[0], 256):
        dm = rounded(dot(w_down[r, :], dy[...]))
        dg[r, :] = (dm * t_in[r, :]).astype(bf16)
        du[r, :] = (dm * s_in[r, :]).astype(bf16)


def b_in(w_gate, w_up, dg, du, h, da):
    total = None
    for r in tiles(da.shape[0], 320):
        d = rounded(dot(w_gate[r, :], dg[...])) + rounded(dot(w_up[r, :], du[...]))
        d = d.astype(bf16)
        da[r, :] = d
        part = jnp.sum(d.astype(f32) * h[r, :].astype(f32), 0, keepdims=True)
        total = part if total is None else total + part
    return total


def b_norm(total, da, h, dy, out):
    wide = h[...].astype(f32)
    scale = inverse_rms(wide)
    k = scale * scale * scale * total * (1.0 / wide.shape[0])
    dh = rounded(da[...].astype(f32) * scale - wide * k)
    out[...] = (dy[...].astype(f32) + dh).astype(bf16)
    h[...] = (wide * scale).astype(bf16)


def kernel(stages, micro, x, dy, w_gate, w_up, w_down, o_gate, o_up, o_down, k_s, k_t, k_mid, k_dg, k_du,
           h_ring, y_ring, acc, st_s, st_t, dg, du, b_send, f_send, a_now, da, stage_in, wg, wu, wd,
           h_sem, y_sem, fs_sem, bs_sem, fo_sem, bi_sem, bo_sem, wi_sem, io_sem):
    me = lax.axis_index("pp")
    first, last = me == 0, me == stages - 1
    n = 2 * micro
    hidden = wd.shape[0]
    half = hidden // 2
    behind = stages - 1 - me
    lead = jnp.where(last, 1, jnp.minimum(4 * behind, n - 2))
    w_lag = jnp.where(lead > n - 5, 3, 0)

    barrier = pltpu.get_barrier_semaphore()

    @pl.when(me > 0)
    def _():
        pl.semaphore_signal(barrier, inc=1, device_id={"pp": me - 1}, device_id_type=MESH)

    @pl.when(me < stages - 1)
    def _():
        pl.semaphore_signal(barrier, inc=1, device_id={"pp": me + 1}, device_id_type=MESH)

    def load(src, c, slot):
        return pltpu.make_async_copy(src.at[c // 2, pl.ds((c % 2) * CHUNK, CHUNK), :], stage_in.at[slot], io_sem.at[slot])

    weights_in = [pltpu.make_async_copy(w.at[0], v, io_sem.at[2 + i]) for i, (w, v) in enumerate(((w_gate, wg), (w_up, wu), (w_down, wd)))]
    for copy in weights_in:
        copy.start()

    @pl.when(first)
    def _():
        load(x, 0, 0).start()
        load(x, 1, 1).start()

    @pl.when(last)
    def _():
        load(dy, 0, 0).start()
        load(dy, 1, 1).start()

    def send_f(c, slot):
        return pltpu.make_async_remote_copy(f_send.at[slot], h_ring.at[c], fs_sem.at[slot], h_sem.at[c], device_id={"pp": me + 1}, device_id_type=MESH)

    def send_b(c, slot):
        return pltpu.make_async_remote_copy(b_send.at[slot], y_ring.at[c], bs_sem.at[slot], y_sem.at[c], device_id={"pp": me - 1}, device_id_type=MESH)

    def keep_st(c):
        return [pltpu.make_async_copy(v.at[c % 2], k.at[c], fo_sem.at[i, c % 2]) for i, (v, k) in enumerate(((st_s, k_s), (st_t, k_t)))]

    def fetch_st(c):
        return [pltpu.make_async_copy(k.at[c], v.at[2 + c % 2], bi_sem.at[i, c % 2]) for i, (v, k) in enumerate(((st_s, k_s), (st_t, k_t)))]

    def keep_d(c):
        return [pltpu.make_async_copy(v.at[c % 2], k.at[c // 2, c % 2], bo_sem.at[i, c % 2]) for i, (v, k) in enumerate(((dg, k_dg), (du, k_du)))]

    def take_x(c):
        @pl.when(first & (c < n))
        def _():
            load(x, c, c % 2).wait()
            transpose_into(h_ring.at[c], stage_in.at[c % 2], CHUNK, wd.shape[1])

            @pl.when(c + 2 < n)
            def _():
                load(x, c + 2, c % 2).start()

    def forward_backward(fwd_refs, cf, cb):
        if cf is not None:
            wgt, wut, wdt, mid = fwd_refs

            def keep_mid(c):
                return pltpu.make_async_copy(mid.at[c % 2], k_mid.at[c // 2, c % 2], fo_sem.at[2, c % 2])

            @pl.when(me > 0)
            def _():
                send_f(cf, cf % 2).wait_recv()

            @pl.when(cf >= 2)
            def _():
                keep_mid(cf - 2).wait()

            @pl.when((cf >= 2) & (me < stages - 1))
            def _():
                send_f(cf - 2, cf % 2).wait_send()
                for copy in keep_st(cf - 2):
                    copy.wait()

        if cb is not None:

            @pl.when(me < stages - 1)
            def _():
                send_b(cb, cb % 2).wait_recv()
                for copy in fetch_st(cb):
                    copy.wait()

                @pl.when(cb + 1 < n)
                def _():
                    for copy in fetch_st(cb + 1):
                        copy.start()

            @pl.when(cb >= 2)
            def _():
                for copy in keep_d(cb - 2):
                    copy.wait()

            @pl.when((cb >= 2) & (me > 0))
            def _():
                send_b(cb - 2, cb % 2).wait_send()

            slot = jnp.where(last, cb % 2, 2 + cb % 2)
            b_mid(wd, y_ring.at[cb], st_s.at[slot], st_t.at[slot], dg.at[cb % 2], du.at[cb % 2])
        if cf is not None:
            f_norm(h_ring.at[cf], a_now, f_send.at[cf % 2])
            f_up(wgt, wut, a_now, st_s.at[cf % 2], st_t.at[cf % 2], mid.at[cf % 2])
        if cb is not None:
            total = b_in(wg, wu, dg.at[cb % 2], du.at[cb % 2], h_ring.at[cb], da)
        if cf is not None:
            f_down(wdt, mid.at[cf % 2], f_send.at[cf % 2])
        if cb is not None:
            b_norm(total, da, h_ring.at[cb], y_ring.at[cb], b_send.at[cb % 2])

        if cb is not None:

            @pl.when(me > 0)
            def _():
                send_b(cb, cb % 2).start()

            for copy in keep_d(cb):
                copy.start()
        if cf is not None:

            @pl.when(me < stages - 1)
            def _():
                send_f(cf, cf % 2).start()
                for copy in keep_st(cf):
                    copy.start()

            keep_mid(cf).start()

    def phase_f(wgt, wut, wdt, mid):
        refs = (wgt, wut, wdt, mid)
        for copy in weights_in:
            copy.wait()
        transpose_into(wgt, wg, *wg.shape)
        transpose_into(wut, wu, *wu.shape)
        transpose_into(wdt, wd, *wd.shape)
        take_x(0)
        pl.semaphore_wait(barrier, jnp.where(first | last, 1, 2))

        @pl.when(last)
        def _():
            def one(c, _):
                load(dy, c, c % 2).wait()
                transpose_into(y_ring.at[c], stage_in.at[c % 2], CHUNK, wd.shape[1])

                @pl.when(c + 2 < n)
                def _():
                    load(dy, c + 2, c % 2).start()

                return 0

            lax.fori_loop(0, n, one, 0)

        def only_f(c, _):
            forward_backward(refs, c, None)
            take_x(c + 1)
            return 0

        lax.fori_loop(0, lead, only_f, 0)
        for block in range(acc.shape[0]):
            acc[block] = jnp.zeros(acc.shape[1:], f32)

        @pl.when(me < stages - 1)
        def _():
            for copy in fetch_st(0):
                copy.start()

        def both(c, _):
            forward_backward(refs, lead + c, c)
            take_x(lead + c + 1)
            return 0

        lax.fori_loop(0, n - lead, both, 0)
        for c in (n - 2, n - 1):
            pltpu.make_async_copy(mid.at[c % 2], k_mid.at[c // 2, c % 2], fo_sem.at[2, c % 2]).wait()

            @pl.when(me < stages - 1)
            def _():
                send_f(c, c % 2).wait_send()
                for copy in keep_st(c):
                    copy.wait()

    rows, ff = w_gate.shape[1:]
    pl.run_scoped(
        phase_f, pltpu.VMEM((ff, rows), bf16), pltpu.VMEM((ff, rows), bf16), pltpu.VMEM((rows, ff), bf16), pltpu.VMEM((2, ff, CHUNK), bf16)
    )

    def phase_w(win):
        def fetch_w(w):
            return [
                pltpu.make_async_copy(k.at[w // 2, :, pl.ds((w % 2) * half, half), :], win.at[w % 3, i], wi_sem.at[w % 3, i])
                for i, k in enumerate((k_dg, k_du, k_mid))
            ]

        def half_w(w):
            for copy in fetch_w(w):
                copy.wait()

            @pl.when(w + 2 < n)
            def _():
                for copy in fetch_w(w + 2):
                    copy.start()

            c = (w // 2) * 2
            per = half // 256
            for i, left in enumerate((h_ring, h_ring, y_ring)):
                for j, r in enumerate(tiles(half, 256)):
                    term = dot_t(left[c], win[w % 3, i, 0, r, :]) + dot_t(left[c + 1], win[w % 3, i, 1, r, :])
                    block = i * 2 * per + (w % 2) * per + j
                    acc[block] += rounded(term)

        @pl.when(w_lag == 0)
        def _():
            for w in range(2):
                for copy in fetch_w(w):
                    copy.start()

        def b_and_w(j, _):
            forward_backward(None, None, n - lead + j)

            @pl.when((w_lag > 0) & (j == 1))
            def _():
                for copy in fetch_w(0):
                    copy.start()

            @pl.when((w_lag > 0) & (j == 2))
            def _():
                for copy in fetch_w(1):
                    copy.start()

            @pl.when(j >= w_lag)
            def _():
                half_w(j - w_lag)

            return 0

        lax.fori_loop(0, lead, b_and_w, 0)
        for c in (n - 2, n - 1):
            for copy in keep_d(c):
                copy.wait()

            @pl.when(me > 0)
            def _():
                send_b(c, c % 2).wait_send()

        def only_w(w, _):
            half_w(w)
            return 0

        lax.fori_loop(lead - w_lag, n, only_w, 0)

    pl.run_scoped(phase_w, pltpu.VMEM((3, 3, 2, half, CHUNK), bf16))
    per = 2 * half // 256
    outs = []
    for i, o in enumerate((o_gate, o_up, o_down)):
        for j, r in enumerate(tiles(hidden, 256)):
            h_ring[i * per + j] = acc[i * per + j].astype(bf16)
            outs.append(pltpu.make_async_copy(h_ring.at[i * per + j], o.at[0, :, r], io_sem.at[5 + i * per + j]))
            outs[-1].start()
    for copy in outs:
        copy.wait()


def solution(mesh):
    stages = mesh.shape["pp"]

    def step(x, dy, w_gate, w_up, w_down):
        micro, d = x.shape[0], x.shape[2]
        ff = w_gate.shape[2]
        n = 2 * micro
        hbm = pl.BlockSpec(memory_space=pltpu.HBM)
        out = jax.ShapeDtypeStruct((1, d, ff), bf16)
        kept = jax.ShapeDtypeStruct((n, ff, CHUNK), f32)
        paired = jax.ShapeDtypeStruct((micro, 2, ff, CHUNK), bf16)
        dma = pltpu.SemaphoreType.DMA
        d_gate, d_up, d_down, *_ = pl.pallas_call(
            functools.partial(kernel, stages, micro),
            out_shape=[out, out, out, kept, kept, paired, paired, paired],
            in_specs=[hbm] * 5,
            out_specs=[hbm] * 8,
            scratch_shapes=[
                pltpu.VMEM((n, d, CHUNK), bf16),
                pltpu.VMEM((n, d, CHUNK), bf16),
                pltpu.VMEM((3 * ff // 256, d, 256), f32),
                pltpu.VMEM((4, ff, CHUNK), f32),
                pltpu.VMEM((4, ff, CHUNK), f32),
                pltpu.VMEM((2, ff, CHUNK), bf16),
                pltpu.VMEM((2, ff, CHUNK), bf16),
                pltpu.VMEM((2, d, CHUNK), bf16),
                pltpu.VMEM((2, d, CHUNK), bf16),
                pltpu.VMEM((d, CHUNK), bf16),
                pltpu.VMEM((d, CHUNK), bf16),
                pltpu.VMEM((2, CHUNK, d), bf16),
                pltpu.VMEM((d, ff), bf16),
                pltpu.VMEM((d, ff), bf16),
                pltpu.VMEM((ff, d), bf16),
                dma((n,)),
                dma((n,)),
                dma((2,)),
                dma((2,)),
                dma((3, 2)),
                dma((2, 2)),
                dma((2, 2)),
                dma((3, 3)),
                dma((5 + 3 * ff // 256,)),
            ],
            compiler_params=pltpu.CompilerParams(collective_id=0, has_side_effects=True, vmem_limit_bytes=67043328),
        )(x, dy, w_gate, w_up, w_down)
        return d_gate, d_up, jnp.swapaxes(d_down, 1, 2)

    return jax.shard_map(
        step,
        mesh=mesh,
        in_specs=(P("rep", None, None),) * 2 + (P("pp", None, None),) * 3,
        out_specs=(P(("rep", "pp"), None, None),) * 3,
        check_vma=False,
    )
```

time: 1240 us -> 268 us (0.22)
  the two profiles are of different devices: /device:TPU:3 before, /device:TPU:28 now
where the time goes in v1:
time: 268 us; the launch traced here: 267 us
  Pallas kernels  259 us (97%)
  local copies, waits for them, and re-layouts  7.65 us (3%)
    pallas_call x1, Pallas kernels, step(): pl.pallas_call(functools.partial(kernel, stages, micro), out_shape=[out,...  259 us
    unnamed x7, local copies, waits for them, and re-layouts  7.65 us

profile of v1, /device:TPU:28, one launch (start us, length us, event | category | flops | bytes accessed | tf_op | source)
XLA Modules:
  0.0 267.2 jit_solution(1324910172904331467)
XLA Ops:
  0.6 259.0 %shard_map.76 = (bf16[1,640,1536]{2,1,0:T(8,128)(2,1)}, bf16[1,640,1536]{2,1,0:T(8,128)(2,1)}, bf16[1,640,1536]{2,1,0:T(8,128)(2,1)}, f32[32,1536,256]{2,1,0:T(8...) custom-call(bf16[16,512,640]{2,1,0:T(8,128)(2,1)} %x.1, ...), custom_call_target="tpu_custom_call" | custom-call | tf_op jit(solution)/shard_map/pallas_call | solution.py:374
  259.6 0.0 copy-start.1
  259.6 4.1 %copy.8 = bf16[1,1536,640]{2,1,0:T(8,128)(2,1)} copy(bf16[1,1536,640]{1,2,0:T(8,128)(2,1)} %bitcast.1) | data formatting | bytes 3932160
  263.7 0.0 copy-done.1
  263.7 0.0 copy-start
  263.7 1.3 copy.11
  265.0 1.0 copy-done
  266.0 1.3 copy.12
Async XLA Ops:
  259.6 4.1 %copy-start.1 = (bf16[1,640,1536]{2,1,0:T(8,128)(2,1)S(1)}, bf16[1,640,1536]{2,1,0:T(8,128)(2,1)}, u32[]{:S(2)}) copy-start(bf16[1,640,1536]{2,1,0:T(8,128)(2,1)} %get-tuple-element.15) | copy-start | bytes 5898244
  263.7 2.3 copy-start

commit v2 on v1

v2 whole, which is shorter than its diff:
```python
import functools

import jax
import jax.numpy as jnp
from jax import lax
from jax.experimental import pallas as pl
from jax.experimental.pallas import tpu as pltpu
from jax.sharding import PartitionSpec as P

f32, bf16 = jnp.float32, jnp.bfloat16
MESH = pl.DeviceIdType.MESH
CHUNK = 256
SENDS = 4
SUB = 64
LEADS = (30, 27, 20, 17, 12, 9, 4, 1)


def dot(a, b):
    return lax.dot_general(a, b, (((1,), (0,)), ((), ())), preferred_element_type=f32)


def dot_t(a, b):
    return lax.dot_general(a, b, (((1,), (1,)), ((), ())), preferred_element_type=f32)


def rounded(v):
    return v.astype(bf16).astype(f32)


def tiles(total, size):
    return [pl.ds(i, size) for i in range(0, total, size)]


def inverse_rms(h):
    total = None
    for r in tiles(h.shape[0], SUB):
        wide = h[r, :].astype(f32)
        total = wide * wide if total is None else total + wide * wide
    return lax.rsqrt(jnp.sum(total, 0, keepdims=True) * (1.0 / h.shape[0]) + 1e-6)


def transpose_into(dst, src, rows, cols):
    for r in tiles(rows, 128):
        for c in tiles(cols, 128):
            dst[c, r] = src[r, c].T


def f_norm(h, a, out):
    scale = inverse_rms(h)
    for r in tiles(h.shape[0], SUB):
        a[r, :] = (h[r, :].astype(f32) * scale).astype(bf16)
        out[r, :] = h[r, :]


def f_up(w_gate, w_up, a, s_out, t_out, mid):
    for r in tiles(mid.shape[0], 256):
        g = dot(w_gate[r, :], a[...])
        u = dot(w_up[r, :], a[...])
        sig = 1.0 / (1.0 + jnp.exp(-g))
        s = g * sig
        s_out[r, :] = s
        t_out[r, :] = u * (sig + s * (1.0 - sig))
        mid[r, :] = (s * u).astype(bf16)


def f_down(w_down, mid, out):
    for r in tiles(out.shape[0], 320):
        out[r, :] += dot(w_down[r, :], mid[...]).astype(bf16)


def b_mid(w_down, dy, s_in, t_in, dg, du):
    for r in tiles(dg.shape[0], 256):
        dm = rounded(dot(w_down[r, :], dy[...]))
        dg[r, :] = (dm * t_in[r, :]).astype(bf16)
        du[r, :] = (dm * s_in[r, :]).astype(bf16)


def b_in(w_gate, w_up, dg, du, h, da):
    total = None
    for r in tiles(da.shape[0], 320):
        d = dot(w_gate[r, :], dg[...]).astype(bf16) + dot(w_up[r, :], du[...]).astype(bf16)
        da[r, :] = d
        part = d.astype(f32) * h[r, :].astype(f32)
        total = part if total is None else total + part
    return jnp.sum(total, 0, keepdims=True)


def b_norm(total, scale, h, dy, out):
    k = scale * scale * scale * total * (1.0 / h.shape[0])
    for q in tiles(h.shape[0], SUB):
        wide = h[q, :].astype(f32)
        dh = out[q, :].astype(f32) * scale - wide * k
        out[q, :] = dy[q, :] + dh.astype(bf16)
        h[q, :] = (wide * scale).astype(bf16)


def w_term(left, right):
    return dot_t(left[0], right[0]) + dot_t(left[1], right[1])


def w_add(acc, term):
    acc[...] += rounded(term)


def odd(i):
    return lax.rem(i, 2)


def half_of(i):
    return lax.div(i, 2)


def kernel(stages, micro, x, dy, w_gate, w_up, w_down, o_gate, o_up, o_down, k_s, k_t, k_mid, k_dg, k_du,
           h_ring, y_ring, dg, du, b_send, f_send, wg, wu, wd,
           h_sem, y_sem, fs_sem, bs_sem, fo_sem, bi_sem, bo_sem, wi_sem, io_sem):
    me = lax.axis_index("pp")
    first, last = me == 0, me == stages - 1
    n = 2 * micro
    hidden = wd.shape[0]
    half = hidden // 2
    lead = sum(jnp.where(me == s, v, 0) for s, v in enumerate(LEADS))
    w_lag = jnp.where(last, 0, jnp.where(lead > n - 5, 3, 1))
    rest = jnp.where(last, 0, lead)

    barrier = pltpu.get_barrier_semaphore()

    @pl.when(me > 0)
    def _():
        pl.semaphore_signal(barrier, inc=1, device_id={"pp": me - 1}, device_id_type=MESH)

    @pl.when(me < stages - 1)
    def _():
        pl.semaphore_signal(barrier, inc=1, device_id={"pp": me + 1}, device_id_type=MESH)

    weights_in = [pltpu.make_async_copy(w.at[0], v, io_sem.at[2 + i]) for i, (w, v) in enumerate(((w_gate, wg), (w_up, wu), (w_down, wd)))]
    for copy in weights_in:
        copy.start()

    def send_f(c):
        return pltpu.make_async_remote_copy(f_send.at[lax.rem(c, SENDS)], h_ring.at[c], fs_sem.at[lax.rem(c, SENDS)], h_sem.at[c], device_id={"pp": me + 1}, device_id_type=MESH)

    def send_b(c):
        return pltpu.make_async_remote_copy(b_send.at[lax.rem(c, SENDS)], y_ring.at[c], bs_sem.at[lax.rem(c, SENDS)], y_sem.at[c], device_id={"pp": me - 1}, device_id_type=MESH)

    def keep_st(st, c):
        return [pltpu.make_async_copy(v.at[odd(c)], k.at[c], fo_sem.at[i, odd(c)]) for i, (v, k) in enumerate(zip(st, (k_s, k_t)))]

    def fetch_st(st, hold, c):
        return [pltpu.make_async_copy(k.at[c], v.at[hold + odd(c)], bi_sem.at[i, odd(c)]) for i, (v, k) in enumerate(zip(st, (k_s, k_t)))]

    def keep_d(c):
        return [pltpu.make_async_copy(v.at[odd(c)], k.at[half_of(c), odd(c)], bo_sem.at[i, odd(c)]) for i, (v, k) in enumerate(((dg, k_dg), (du, k_du)))]

    def forward_backward(st, hold, until, cf, cb, fwd_refs=None, w=None, w_open=None, w_tiles=None):
        if cf is not None:
            wgt, wut, wdt, mid, a_now = fwd_refs

            def keep_mid(c):
                return pltpu.make_async_copy(mid.at[odd(c)], k_mid.at[half_of(c), odd(c)], fo_sem.at[2, odd(c)])

            @pl.when(me > 0)
            def _():
                with jax.named_scope("wait_h"):
                    send_f(cf).wait_recv()

            @pl.when(cf >= 2)
            def _():
                keep_mid(cf - 2).wait()

            @pl.when((cf >= 2) & (me < stages - 1))
            def _():
                for copy in keep_st(st, cf - 2):
                    copy.wait()

            @pl.when((cf >= SENDS) & (me < stages - 1))
            def _():
                with jax.named_scope("wait_fs"):
                    send_f(cf - SENDS).wait_send()

        if cb is not None:

            @pl.when(me < stages - 1)
            def _():
                with jax.named_scope("wait_y"):
                    send_b(cb).wait_recv()
                with jax.named_scope("wait_st"):
                    for copy in fetch_st(st, hold, cb):
                        copy.wait()

                @pl.when(cb + 1 < until)
                def _():
                    for copy in fetch_st(st, hold, cb + 1):
                        copy.start()

            @pl.when(cb >= 2)
            def _():
                with jax.named_scope("wait_d"):
                    for copy in keep_d(cb - 2):
                        copy.wait()

            @pl.when((cb >= SENDS) & (me > 0))
            def _():
                with jax.named_scope("wait_bs"):
                    send_b(cb - SENDS).wait_send()

        if w is not None:
            with jax.named_scope("wait_w"):
                w_open(w)
        with jax.named_scope(("F" if cf is not None else "") + ("B" if cb is not None else "") + ("W" if w is not None else "")):
            if cb is not None:
                slot, out = hold + odd(cb), b_send.at[lax.rem(cb, SENDS)]
                b_mid(wd, y_ring.at[cb], st[0].at[slot], st[1].at[slot], dg.at[odd(cb)], du.at[odd(cb)])
                scale = inverse_rms(h_ring.at[cb])
            if w is not None:
                for tile in w_tiles[: len(w_tiles) // 2]:
                    tile(w)
            if cf is not None:
                f_norm(h_ring.at[cf], a_now, f_send.at[lax.rem(cf, SENDS)])
                f_up(wgt, wut, a_now, st[0].at[odd(cf)], st[1].at[odd(cf)], mid.at[odd(cf)])
            if cb is not None:
                total = b_in(wg, wu, dg.at[odd(cb)], du.at[odd(cb)], h_ring.at[cb], out)
            if cf is not None:
                f_down(wdt, mid.at[odd(cf)], f_send.at[lax.rem(cf, SENDS)])
            if w is not None:
                for tile in w_tiles[len(w_tiles) // 2 :]:
                    tile(w)
            if cb is not None:
                b_norm(total, scale, h_ring.at[cb], y_ring.at[cb], out)

        if cb is not None:

            @pl.when(me > 0)
            def _():
                send_b(cb).start()

        if cf is not None:

            @pl.when(me < stages - 1)
            def _():
                send_f(cf).start()
                for copy in keep_st(st, cf):
                    copy.start()

            keep_mid(cf).start()
        if cb is not None:
            for copy in keep_d(cb):
                copy.start()

    def phase_f(st_s, st_t, wgt, wut, wdt, mid, a_now, stage_in):
        def load(src, c, slot):
            return pltpu.make_async_copy(src.at[half_of(c), pl.ds(odd(c) * CHUNK, CHUNK), :], stage_in.at[slot], io_sem.at[slot])

        def take_x(c):
            @pl.when(first & (c < n))
            def _():
                load(x, c, odd(c)).wait()
                transpose_into(h_ring.at[c], stage_in.at[odd(c)], CHUNK, wd.shape[1])

                @pl.when(c + 2 < n)
                def _():
                    load(x, c + 2, odd(c)).start()

        @pl.when(first)
        def _():
            load(x, 0, 0).start()
            load(x, 1, 1).start()

        @pl.when(last)
        def _():
            load(dy, 0, 0).start()
            load(dy, 1, 1).start()

        refs = (wgt, wut, wdt, mid, a_now)
        st = (st_s, st_t)
        hold = jnp.where(last, 0, 2)

        for copy, turned, w in zip(weights_in, (wgt, wut, wdt), (wg, wu, wd), strict=True):
            copy.wait()
            transpose_into(turned, w, *w.shape)
        take_x(0)
        pl.semaphore_wait(barrier, jnp.where(first | last, 1, 2))

        @pl.when(last)
        def _():
            def one(c, _):
                load(dy, c, odd(c)).wait()
                transpose_into(y_ring.at[c], stage_in.at[odd(c)], CHUNK, wd.shape[1])

                @pl.when(c + 2 < n)
                def _():
                    load(dy, c + 2, odd(c)).start()

                return 0

            lax.fori_loop(0, n, one, 0)

        def only_f(c, _):
            forward_backward(st, hold, n, c, None, refs)

            @pl.when((c == 2) & (me < stages - 1))
            def _():
                for copy in fetch_st(st, hold, 0):
                    copy.start()

            take_x(c + 1)
            return 0

        lax.fori_loop(0, lead, only_f, 0)

        def both(c, _):
            forward_backward(st, hold, n - lead, lead + c, c, refs)
            take_x(lead + c + 1)
            return 0

        lax.fori_loop(0, n - lead, both, 0)

        def only_b(c, _):
            forward_backward(st, hold, n, None, c)
            return 0

        lax.fori_loop(n - lead, n - rest, only_b, 0)
        for c in (n - 2, n - 1):
            pltpu.make_async_copy(mid.at[odd(c)], k_mid.at[half_of(c), odd(c)], fo_sem.at[2, odd(c)]).wait()

            @pl.when(me < stages - 1)
            def _():
                for copy in keep_st(st, c):
                    copy.wait()

    rows, ff = w_gate.shape[1:]
    shapes = (ff, rows), (ff, rows), (rows, ff), (2, ff, CHUNK), (rows, CHUNK), (2, CHUNK, rows)
    wide = pltpu.VMEM((4, ff, CHUNK), f32)
    pl.run_scoped(phase_f, wide, wide, *(pltpu.VMEM(shape, bf16) for shape in shapes))
    per = hidden // 256

    def phase_w(st_s, st_t, acc, win):
        st = (st_s, st_t)

        def fetch_w(w):
            return [
                pltpu.make_async_copy(k.at[half_of(w), :, pl.ds((odd(w)) * half, half), :], win.at[lax.rem(w, 4), i], wi_sem.at[lax.rem(w, 4), i])
                for i, k in enumerate((k_dg, k_du, k_mid))
            ]

        def open_half(w):
            for copy in fetch_w(w):
                copy.wait()

            @pl.when(w + 2 < n)
            def _():
                for copy in fetch_w(w + 2):
                    copy.start()

        def term_of(i, m, slot, j):
            left = (h_ring, h_ring, y_ring)[i]
            r = pl.ds(j * 256, 256)
            return w_term([left[2 * m], left[2 * m + 1]], [win[slot, i, 0, r, :], win[slot, i, 1, r, :]])

        def half_tile(i, j):
            def add(w):
                w_add(acc.at[i * per + (odd(w)) * (per // 2) + j], term_of(i, half_of(w), lax.rem(w, 4), j))

            return add

        half_tiles = [half_tile(i, j) for i in range(3) for j in range(per // 2)]

        @pl.when(rest > 0)
        def _():
            for copy in fetch_st(st, 0, n - rest):
                copy.start()

        @pl.when(w_lag < 2)
        def _():
            for w in range(2):
                for copy in fetch_w(w):
                    copy.start()

        for block in range(acc.shape[0]):
            acc[block] = jnp.zeros(acc.shape[1:], f32)

        def only_b(j, _):
            forward_backward(st, 0, n, None, n - rest + j)

            @pl.when((j > 0) & (w_lag > 1))
            def _():
                for copy in fetch_w(j - 1):
                    copy.start()

            return 0

        lax.fori_loop(0, w_lag, only_b, 0)

        def b_and_w(j, _):
            forward_backward(st, 0, n, None, n - rest + j, None, j - w_lag, open_half, half_tiles)
            return 0

        lax.fori_loop(w_lag, rest, b_and_w, 0)
        for c in (n - 2, n - 1):
            for copy in keep_d(c):
                copy.wait()

        done = rest - w_lag

        @pl.when(odd(done) == 1)
        def _():
            open_half(done)
            for tile in half_tiles:
                tile(done)

        def open_whole(m):
            with jax.named_scope("wait_w"):
                for w in (2 * m, 2 * m + 1):
                    for copy in fetch_w(w):
                        copy.wait()

        def whole_w(m, _):
            open_whole(m)
            for w in (2 * m + 2, 2 * m + 3):
                for copy in fetch_w(w):
                    copy.start()
            with jax.named_scope("WW"):
                for i, j in ((i, j) for i in range(3) for j in range(per)):
                    w_add(acc.at[i * per + j], term_of(i, m, 2 * odd(m) + j // (per // 2), j % (per // 2)))
            return 0

        lax.fori_loop((done + 1) // 2, micro - 1, whole_w, 0)

        m = micro - 1
        open_whole(m)
        outs = []
        for i, o in enumerate((o_gate, o_up, o_down)):
            for j in range(per):
                term = term_of(i, m, 2 * odd(m) + j // (per // 2), j % (per // 2))
                at = i * per + j
                h_ring[at] = (acc[at] + rounded(term)).astype(bf16)
                outs.append(pltpu.make_async_copy(h_ring.at[at], o.at[0, :, pl.ds(j * 256, 256)], io_sem.at[5 + at]))
            for copy in outs[-per:]:
                copy.start()
        with jax.named_scope("out"):
            for copy in outs:
                copy.wait()

    held = pltpu.VMEM((2, ff, CHUNK), f32)
    pl.run_scoped(phase_w, held, held, pltpu.VMEM((3 * per, rows, 256), f32), pltpu.VMEM((4, 3, 2, half, CHUNK), bf16))
    for c in range(n - SENDS, n):

        @pl.when(me < stages - 1)
        def _():
            send_f(c).wait_send()

        @pl.when(me > 0)
        def _():
            send_b(c).wait_send()


def solution(mesh):
    stages = mesh.shape["pp"]

    def step(x, dy, w_gate, w_up, w_down):
        micro, d = x.shape[0], x.shape[2]
        ff = w_gate.shape[2]
        n = 2 * micro
        hbm = pl.BlockSpec(memory_space=pltpu.HBM)
        out = jax.ShapeDtypeStruct((1, d, ff), bf16)
        kept = jax.ShapeDtypeStruct((n, ff, CHUNK), f32)
        paired = jax.ShapeDtypeStruct((micro, 2, ff, CHUNK), bf16)
        dma = pltpu.SemaphoreType.DMA
        d_gate, d_up, d_down, *_ = pl.pallas_call(
            functools.partial(kernel, stages, micro),
            out_shape=[out, out, out, kept, kept, paired, paired, paired],
            in_specs=[hbm] * 5,
            out_specs=[hbm] * 8,
            scratch_shapes=[
                pltpu.VMEM((n, d, CHUNK), bf16),
                pltpu.VMEM((n, d, CHUNK), bf16),
                pltpu.VMEM((2, ff, CHUNK), bf16),
                pltpu.VMEM((2, ff, CHUNK), bf16),
                pltpu.VMEM((SENDS, d, CHUNK), bf16),
                pltpu.VMEM((SENDS, d, CHUNK), bf16),
                pltpu.VMEM((d, ff), bf16),
                pltpu.VMEM((d, ff), bf16),
                pltpu.VMEM((ff, d), bf16),
                dma((n,)),
                dma((n,)),
                dma((SENDS,)),
                dma((SENDS,)),
                dma((3, 2)),
                dma((2, 2)),
                dma((2, 2)),
                dma((4, 3)),
                dma((5 + 3 * ff // 256,)),
            ],
            compiler_params=pltpu.CompilerParams(collective_id=0, has_side_effects=True, vmem_limit_bytes=67043328),
        )(x, dy, w_gate, w_up, w_down)
        return d_gate, d_up, jnp.swapaxes(d_down, 1, 2)

    return jax.shard_map(
        step,
        mesh=mesh,
        in_specs=(P("rep", None, None),) * 2 + (P("pp", None, None),) * 3,
        out_specs=(P(("rep", "pp"), None, None),) * 3,
        check_vma=False,
    )
```

time: 268 us -> 243 us (0.907)
  the two profiles are of different devices: /device:TPU:28 before, /device:TPU:3 now
where the time goes in v2:
time: 243 us; the launch traced here: 239 us
  Pallas kernels  231 us (95%)
  local copies, waits for them, and re-layouts  7.65 us (3%)
    pallas_call x1, Pallas kernels, step(): pl.pallas_call(functools.partial(kernel, stages, micro), out_shape=[out,...  231 us
    unnamed x7, local copies, waits for them, and re-layouts  7.65 us

profile of v2, /device:TPU:3, one launch (start us, length us, event | category | flops | bytes accessed | tf_op | source)
XLA Modules:
  0.0 239.1 jit_solution(3200205071159492213)
XLA Ops:
  0.6 230.8 %shard_map.76 = (bf16[1,640,1536]{2,1,0:T(8,128)(2,1)}, bf16[1,640,1536]{2,1,0:T(8,128)(2,1)}, bf16[1,640,1536]{2,1,0:T(8,128)(2,1)}, f32[32,1536,256]{2,1,0:T(8...) custom-call(bf16[16,512,640]{2,1,0:T(8,128)(2,1)} %x.1, ...), custom_call_target="tpu_custom_call" | custom-call | tf_op jit(solution)/shard_map/pallas_call | solution.py:468
  231.4 0.0 copy-start.1
  231.4 4.1 %copy.8 = bf16[1,1536,640]{2,1,0:T(8,128)(2,1)} copy(bf16[1,1536,640]{1,2,0:T(8,128)(2,1)} %bitcast.1) | data formatting | bytes 3932160
  235.6 0.0 copy-done.1
  235.6 0.0 copy-start
  235.6 1.3 copy.11
  236.8 1.0 copy-done
  237.8 1.3 copy.12
Async XLA Ops:
  231.4 4.1 %copy-start.1 = (bf16[1,640,1536]{2,1,0:T(8,128)(2,1)S(1)}, bf16[1,640,1536]{2,1,0:T(8,128)(2,1)}, u32[]{:S(2)}) copy-start(bf16[1,640,1536]{2,1,0:T(8,128)(2,1)} %get-tuple-element.15) | copy-start | bytes 5898244
  235.6 2.3 copy-start

commit v3 on v2

--- a/solution.py
+++ b/solution.py
@@ -10,9 +10,9 @@
 f32, bf16 = jnp.float32, jnp.bfloat16
 MESH = pl.DeviceIdType.MESH
 CHUNK = 256
-SENDS = 4
+SENDS = 5
 SUB = 64
-LEADS = (30, 27, 20, 17, 12, 9, 4, 1)
+LEADS = (32, 25, 20, 17, 12, 9, 4, 1)
 
 
 def dot(a, b):
@@ -29,13 +29,21 @@
 
 def tiles(total, size):
     return [pl.ds(i, size) for i in range(0, total, size)]
+
+
+def folded(v):
+    while v.shape[0] > 8:
+        rows = v.shape[0] // 2
+        v = v[:rows] + v[rows:]
+    return v
 
 
 def inverse_rms(h):
     total = None
     for r in tiles(h.shape[0], SUB):
         wide = h[r, :].astype(f32)
-        total = wide * wide if total is None else total + wide * wide
+        part = folded(wide * wide)
+        total = part if total is None else total + part
     return lax.rsqrt(jnp.sum(total, 0, keepdims=True) * (1.0 / h.shape[0]) + 1e-6)
 
 
@@ -54,34 +62,44 @@
 
 def f_up(w_gate, w_up, a, s_out, t_out, mid):
     for r in tiles(mid.shape[0], 256):
-        g = dot(w_gate[r, :], a[...])
-        u = dot(w_up[r, :], a[...])
-        sig = 1.0 / (1.0 + jnp.exp(-g))
-        s = g * sig
-        s_out[r, :] = s
-        t_out[r, :] = u * (sig + s * (1.0 - sig))
-        mid[r, :] = (s * u).astype(bf16)
+        gate = dot(w_gate[r, :], a[...])
+        up = dot(w_up[r, :], a[...])
+        for i in range(0, 256, SUB):
+            g, u, q = gate[i : i + SUB], up[i : i + SUB], pl.ds(r.start + i, SUB)
+            sig = 1.0 / (1.0 + jnp.exp(-g))
+            s = g * sig
+            s_out[q, :] = s
+            t_out[q, :] = u * (sig + s * (1.0 - sig))
+            mid[q, :] = (s * u).astype(bf16)
 
 
 def f_down(w_down, mid, out):
     for r in tiles(out.shape[0], 320):
-        out[r, :] += dot(w_down[r, :], mid[...]).astype(bf16)
+        o = dot(w_down[r, :], mid[...])
+        for i in range(0, 320, SUB):
+            out[pl.ds(r.start + i, SUB), :] += o[i : i + SUB].astype(bf16)
 
 
 def b_mid(w_down, dy, s_in, t_in, dg, du):
     for r in tiles(dg.shape[0], 256):
-        dm = rounded(dot(w_down[r, :], dy[...]))
-        dg[r, :] = (dm * t_in[r, :]).astype(bf16)
-        du[r, :] = (dm * s_in[r, :]).astype(bf16)
+        d = dot(w_down[r, :], dy[...])
+        for i in range(0, 256, SUB):
+            dm, q = rounded(d[i : i + SUB]), pl.ds(r.start + i, SUB)
+            dg[q, :] = (dm * t_in[q, :]).astype(bf16)
+            du[q, :] = (dm * s_in[q, :]).astype(bf16)
 
 
 def b_in(w_gate, w_up, dg, du, h, da):
     total = None
     for r in tiles(da.shape[0], 320):
-        d = dot(w_gate[r, :], dg[...]).astype(bf16) + dot(w_up[r, :], du[...]).astype(bf16)
-        da[r, :] = d
-        part = d.astype(f32) * h[r, :].astype(f32)
-        total = part if total is None else total + part
+        by_gate = dot(w_gate[r, :], dg[...])
+        by_up = dot(w_up[r, :], du[...])
+        for i in range(0, 320, SUB):
+            q = pl.ds(r.start + i, SUB)
+            d = by_gate[i : i + SUB].astype(bf16) + by_up[i : i + SUB].astype(bf16)
+            da[q, :] = d
+            part = folded(d.astype(f32) * h[q, :].astype(f32))
+            total = part if total is None else total + part
     return jnp.sum(total, 0, keepdims=True)
 
 
@@ -111,15 +129,15 @@
 
 
 def kernel(stages, micro, x, dy, w_gate, w_up, w_down, o_gate, o_up, o_down, k_s, k_t, k_mid, k_dg, k_du,
-           h_ring, y_ring, dg, du, b_send, f_send, wg, wu, wd,
-           h_sem, y_sem, fs_sem, bs_sem, fo_sem, bi_sem, bo_sem, wi_sem, io_sem):
+           h_ring, y_ring, dg, du, sends, wg, wu, wd,
+           h_sem, y_sem, send_sem, fo_sem, bi_sem, bo_sem, wi_sem, io_sem):
     me = lax.axis_index("pp")
     first, last = me == 0, me == stages - 1
     n = 2 * micro
     hidden = wd.shape[0]
     half = hidden // 2
     lead = sum(jnp.where(me == s, v, 0) for s, v in enumerate(LEADS))
-    w_lag = jnp.where(last, 0, jnp.where(lead > n - 5, 3, 1))
+    w_lag = jnp.where(last, 0, jnp.where(lead > n - 5, 4, 1))
     rest = jnp.where(last, 0, lead)
 
     barrier = pltpu.get_barrier_semaphore()
@@ -133,14 +151,25 @@
         pl.semaphore_signal(barrier, inc=1, device_id={"pp": me + 1}, device_id_type=MESH)
 
     weights_in = [pltpu.make_async_copy(w.at[0], v, io_sem.at[2 + i]) for i, (w, v) in enumerate(((w_gate, wg), (w_up, wu), (w_down, wd)))]
-    for copy in weights_in:
+    for copy in weights_in[:2]:
         copy.start()
 
+    f_places = jnp.where(odd(me) == 1, SENDS - 2, 2)
+    b_places = SENDS - f_places
+
+    def f_place(c):
+        return lax.rem(c, f_places)
+
+    def b_place(c):
+        return f_places + lax.rem(c, b_places)
+
     def send_f(c):
-        return pltpu.make_async_remote_copy(f_send.at[lax.rem(c, SENDS)], h_ring.at[c], fs_sem.at[lax.rem(c, SENDS)], h_sem.at[c], device_id={"pp": me + 1}, device_id_type=MESH)
+        place = f_place(c)
+        return pltpu.make_async_remote_copy(sends.at[place], h_ring.at[c], send_sem.at[place], h_sem.at[c], device_id={"pp": me + 1}, device_id_type=MESH)
 
     def send_b(c):
-        return pltpu.make_async_remote_copy(b_send.at[lax.rem(c, SENDS)], y_ring.at[c], bs_sem.at[lax.rem(c, SENDS)], y_sem.at[c], device_id={"pp": me - 1}, device_id_type=MESH)
+        place = b_place(c)
+        return pltpu.make_async_remote_copy(sends.at[place], y_ring.at[c], send_sem.at[place], y_sem.at[c], device_id={"pp": me - 1}, device_id_type=MESH)
 
     def keep_st(st, c):
         return [pltpu.make_async_copy(v.at[odd(c)], k.at[c], fo_sem.at[i, odd(c)]) for i, (v, k) in enumerate(zip(st, (k_s, k_t)))]
@@ -172,10 +201,10 @@
                 for copy in keep_st(st, cf - 2):
                     copy.wait()
 
-            @pl.when((cf >= SENDS) & (me < stages - 1))
+            @pl.when((cf >= f_places) & (me < stages - 1))
             def _():
                 with jax.named_scope("wait_fs"):
-                    send_f(cf - SENDS).wait_send()
+                    send_f(cf - f_places).wait_send()
 
         if cb is not None:
 
@@ -198,34 +227,34 @@
                     for copy in keep_d(cb - 2):
                         copy.wait()
 
-            @pl.when((cb >= SENDS) & (me > 0))
+            @pl.when((cb >= b_places) & (me > 0))
             def _():
                 with jax.named_scope("wait_bs"):
-                    send_b(cb - SENDS).wait_send()
+                    send_b(cb - b_places).wait_send()
 
         if w is not None:
             with jax.named_scope("wait_w"):
                 w_open(w)
         with jax.named_scope(("F" if cf is not None else "") + ("B" if cb is not None else "") + ("W" if w is not None else "")):
             if cb is not None:
-                slot, out = hold + odd(cb), b_send.at[lax.rem(cb, SENDS)]
+                slot, out = hold + odd(cb), sends.at[b_place(cb)]
                 b_mid(wd, y_ring.at[cb], st[0].at[slot], st[1].at[slot], dg.at[odd(cb)], du.at[odd(cb)])
                 scale = inverse_rms(h_ring.at[cb])
             if w is not None:
                 for tile in w_tiles[: len(w_tiles) // 2]:
                     tile(w)
             if cf is not None:
-                f_norm(h_ring.at[cf], a_now, f_send.at[lax.rem(cf, SENDS)])
+                f_norm(h_ring.at[cf], a_now, sends.at[f_place(cf)])
                 f_up(wgt, wut, a_now, st[0].at[odd(cf)], st[1].at[odd(cf)], mid.at[odd(cf)])
             if cb is not None:
                 total = b_in(wg, wu, dg.at[odd(cb)], du.at[odd(cb)], h_ring.at[cb], out)
-            if cf is not None:
-                f_down(wdt, mid.at[odd(cf)], f_send.at[lax.rem(cf, SENDS)])
             if w is not None:
                 for tile in w_tiles[len(w_tiles) // 2 :]:
                     tile(w)
             if cb is not None:
                 b_norm(total, scale, h_ring.at[cb], y_ring.at[cb], out)
+            if cf is not None:
+                f_down(wdt, mid.at[odd(cf)], sends.at[f_place(cf)])
 
         if cb is not None:
 
@@ -274,8 +303,10 @@
         st = (st_s, st_t)
         hold = jnp.where(last, 0, 2)
 
-        for copy, turned, w in zip(weights_in, (wgt, wut, wdt), (wg, wu, wd), strict=True):
-            copy.wait()
+        for i, (turned, w) in enumerate(((wgt, wg), (wut, wu), (wdt, wd))):
+            weights_in[i].wait()
+            if i == 0:
+                weights_in[2].start()
             transpose_into(turned, w, *w.shape)
         take_x(0)
         pl.semaphore_wait(barrier, jnp.where(first | last, 1, 2))
@@ -297,7 +328,7 @@
         def only_f(c, _):
             forward_backward(st, hold, n, c, None, refs)
 
-            @pl.when((c == 2) & (me < stages - 1))
+            @pl.when((c == 2) & (lead < n) & (me < stages - 1))
             def _():
                 for copy in fetch_st(st, hold, 0):
                     copy.start()
@@ -346,10 +377,8 @@
             for copy in fetch_w(w):
                 copy.wait()
 
-            @pl.when(w + 2 < n)
-            def _():
-                for copy in fetch_w(w + 2):
-                    copy.start()
+            for copy in fetch_w(w + 1):
+                copy.start()
 
         def term_of(i, m, slot, j):
             left = (h_ring, h_ring, y_ring)[i]
@@ -371,9 +400,13 @@
 
         @pl.when(w_lag < 2)
         def _():
-            for w in range(2):
-                for copy in fetch_w(w):
-                    copy.start()
+            for copy in fetch_w(0):
+                copy.start()
+
+        @pl.when(last)
+        def _():
+            for copy in fetch_w(1):
+                copy.start()
 
         for block in range(acc.shape[0]):
             acc[block] = jnp.zeros(acc.shape[1:], f32)
@@ -381,9 +414,9 @@
         def only_b(j, _):
             forward_backward(st, 0, n, None, n - rest + j)
 
-            @pl.when((j > 0) & (w_lag > 1))
-            def _():
-                for copy in fetch_w(j - 1):
+            @pl.when((w_lag > 1) & (j == w_lag - 1))
+            def _():
+                for copy in fetch_w(0):
                     copy.start()
 
             return 0
@@ -406,6 +439,11 @@
             open_half(done)
             for tile in half_tiles:
                 tile(done)
+
+        @pl.when(jnp.logical_not(last))
+        def _():
+            for copy in fetch_w(2 * half_of(done + 1) + 1):
+                copy.start()
 
         def open_whole(m):
             with jax.named_scope("wait_w"):
@@ -423,34 +461,48 @@
                     w_add(acc.at[i * per + j], term_of(i, m, 2 * odd(m) + j // (per // 2), j % (per // 2)))
             return 0
 
-        lax.fori_loop((done + 1) // 2, micro - 1, whole_w, 0)
+        lax.fori_loop(half_of(done + 1), micro - 1, whole_w, 0)
 
         m = micro - 1
         open_whole(m)
-        outs = []
-        for i, o in enumerate((o_gate, o_up, o_down)):
+
+        def finish(i, take):
             for j in range(per):
-                term = term_of(i, m, 2 * odd(m) + j // (per // 2), j % (per // 2))
-                at = i * per + j
-                h_ring[at] = (acc[at] + rounded(term)).astype(bf16)
-                outs.append(pltpu.make_async_copy(h_ring.at[at], o.at[0, :, pl.ds(j * 256, 256)], io_sem.at[5 + at]))
-            for copy in outs[-per:]:
-                copy.start()
-        with jax.named_scope("out"):
-            for copy in outs:
-                copy.wait()
+                take(j, (acc[i * per + j] + rounded(term_of(i, m, 2 * odd(m) + j // (per // 2), j % (per // 2)))).astype(bf16))
+
+        def take_down(j, v):
+            h_ring[j] = v
+
+        def take_gate(j, v):
+            o_gate[0, :, j * 256 : (j + 1) * 256] = v
+
+        def take_up(j, v):
+            o_up[0, :, j * 256 : (j + 1) * 256] = v
+
+        finish(2, take_down)
+        finish(0, take_gate)
+        for j in range(per):
+            transpose_into(o_down.at[0, pl.ds(j * 256, 256), :], h_ring.at[j], rows, 256)
+        finish(1, take_up)
 
     held = pltpu.VMEM((2, ff, CHUNK), f32)
     pl.run_scoped(phase_w, held, held, pltpu.VMEM((3 * per, rows, 256), f32), pltpu.VMEM((4, 3, 2, half, CHUNK), bf16))
-    for c in range(n - SENDS, n):
-
-        @pl.when(me < stages - 1)
-        def _():
+
+    @pl.when(me < stages - 1)
+    def _():
+        def sent(c, _):
             send_f(c).wait_send()
-
-        @pl.when(me > 0)
-        def _():
+            return 0
+
+        lax.fori_loop(n - f_places, n, sent, 0)
+
+    @pl.when(me > 0)
+    def _():
+        def sent(c, _):
             send_b(c).wait_send()
+            return 0
+
+        lax.fori_loop(n - b_places, n, sent, 0)
 
 
 def solution(mesh):
@@ -461,21 +513,20 @@
         ff = w_gate.shape[2]
         n = 2 * micro
         hbm = pl.BlockSpec(memory_space=pltpu.HBM)
-        out = jax.ShapeDtypeStruct((1, d, ff), bf16)
+        out = pltpu.VMEM((1, d, ff), bf16)
         kept = jax.ShapeDtypeStruct((n, ff, CHUNK), f32)
         paired = jax.ShapeDtypeStruct((micro, 2, ff, CHUNK), bf16)
         dma = pltpu.SemaphoreType.DMA
         d_gate, d_up, d_down, *_ = pl.pallas_call(
             functools.partial(kernel, stages, micro),
-            out_shape=[out, out, out, kept, kept, paired, paired, paired],
+            out_shape=[out, out, pltpu.VMEM((1, ff, d), bf16), kept, kept, paired, paired, paired],
             in_specs=[hbm] * 5,
-            out_specs=[hbm] * 8,
+            out_specs=[pl.BlockSpec(memory_space=pltpu.VMEM)] * 3 + [hbm] * 5,
             scratch_shapes=[
                 pltpu.VMEM((n, d, CHUNK), bf16),
                 pltpu.VMEM((n, d, CHUNK), bf16),
                 pltpu.VMEM((2, ff, CHUNK), bf16),
                 pltpu.VMEM((2, ff, CHUNK), bf16),
-                pltpu.VMEM((SENDS, d, CHUNK), bf16),
                 pltpu.VMEM((SENDS, d, CHUNK), bf16),
                 pltpu.VMEM((d, ff), bf16),
                 pltpu.VMEM((d, ff), bf16),
@@ -483,16 +534,15 @@
                 dma((n,)),
                 dma((n,)),
                 dma((SENDS,)),
-                dma((SENDS,)),
                 dma((3, 2)),
                 dma((2, 2)),
                 dma((2, 2)),
                 dma((4, 3)),
-                dma((5 + 3 * ff // 256,)),
+                dma((5,)),
             ],
-            compiler_params=pltpu.CompilerParams(collective_id=0, has_side_effects=True, vmem_limit_bytes=67043328),
+            compiler_params=pltpu.CompilerParams(collective_id=0, has_side_effects=True, vmem_limit_bytes=61100000),
         )(x, dy, w_gate, w_up, w_down)
-        return d_gate, d_up, jnp.swapaxes(d_down, 1, 2)
+        return d_gate, d_up, d_down
 
     return jax.shard_map(
         step,

time: 243 us -> 239 us (0.984); the launches traced: 239 us -> 238 us
  local copies, waits for them, and re-layouts: 7.65 us -> 3.82 us
  Pallas kernels: 231 us -> 234 us
    unnamed x7 -> x3, local copies, waits for them, and re-layouts: 7.65 us -> 3.82 us
    pallas_call x1, Pallas kernels: 231 us -> 234 us  [step(): pl.pallas_call(functools.partial(kernel, stages, micro), out_shape=[out,...]
where the time goes in v3:
time: 239 us; the launch traced here: 238 us
  Pallas kernels  234 us (98%)
  local copies, waits for them, and re-layouts  3.82 us (2%)
    pallas_call x1, Pallas kernels, step(): pl.pallas_call(functools.partial(kernel, stages, micro), out_shape=[out,...  234 us

profile of v3, /device:TPU:3, one launch (start us, length us, event | category | flops | bytes accessed | tf_op | source)
XLA Modules:
  0.0 238.3 jit_solution(3744972277577782415)
XLA Ops:
  0.6 233.8 %shard_map.76 = (bf16[1,640,1536]{2,1,0:T(8,128)(2,1)S(1)}, bf16[1,640,1536]{2,1,0:T(8,128)(2,1)S(1)}, bf16[1,1536,640]{2,1,0:T(8,128)(2,1)S(1)}, f32[32,1536,25...) custom-call(bf16[16,512,640]{2,1,0:T(8,128)(2,1)} %x.1, ...), custom_call_target="tpu_custom_call" | custom-call | tf_op jit(solution)/shard_map/pallas_call | solution.py:520
  234.5 1.3 copy.11
  235.7 1.3 copy.12
  237.0 1.3 copy.13

commit v4 on v3

--- a/solution.py
+++ b/solution.py
@@ -137,8 +137,8 @@
     hidden = wd.shape[0]
     half = hidden // 2
     lead = sum(jnp.where(me == s, v, 0) for s, v in enumerate(LEADS))
-    w_lag = jnp.where(last, 0, jnp.where(lead > n - 5, 4, 1))
-    rest = jnp.where(last, 0, lead)
+    rest = lead - 1
+    w_lag = jnp.where(last, 0, jnp.where(rest > n - 5, 3, 1))
 
     barrier = pltpu.get_barrier_semaphore()
 
@@ -151,7 +151,7 @@
         pl.semaphore_signal(barrier, inc=1, device_id={"pp": me + 1}, device_id_type=MESH)
 
     weights_in = [pltpu.make_async_copy(w.at[0], v, io_sem.at[2 + i]) for i, (w, v) in enumerate(((w_gate, wg), (w_up, wu), (w_down, wd)))]
-    for copy in weights_in[:2]:
+    for copy in weights_in:
         copy.start()
 
     f_places = jnp.where(odd(me) == 1, SENDS - 2, 2)
@@ -305,8 +305,6 @@
 
         for i, (turned, w) in enumerate(((wgt, wg), (wut, wu), (wdt, wd))):
             weights_in[i].wait()
-            if i == 0:
-                weights_in[2].start()
             transpose_into(turned, w, *w.shape)
         take_x(0)
         pl.semaphore_wait(barrier, jnp.where(first | last, 1, 2))
@@ -328,7 +326,7 @@
         def only_f(c, _):
             forward_backward(st, hold, n, c, None, refs)
 
-            @pl.when((c == 2) & (lead < n) & (me < stages - 1))
+            @pl.when((c == 2) & (me < stages - 1))
             def _():
                 for copy in fetch_st(st, hold, 0):
                     copy.start()
@@ -339,14 +337,14 @@
         lax.fori_loop(0, lead, only_f, 0)
 
         def both(c, _):
-            forward_backward(st, hold, n - lead, lead + c, c, refs)
+            forward_backward(st, hold, n - rest, lead + c, c, refs)
             take_x(lead + c + 1)
             return 0
 
         lax.fori_loop(0, n - lead, both, 0)
 
         def only_b(c, _):
-            forward_backward(st, hold, n, None, c)
+            forward_backward(st, hold, n - rest, None, c)
             return 0
 
         lax.fori_loop(n - lead, n - rest, only_b, 0)
@@ -373,12 +371,17 @@
                 for i, k in enumerate((k_dg, k_du, k_mid))
             ]
 
+        def fetch_pair(w):
+            for copy in fetch_w(w) + fetch_w(w + 1):
+                copy.start()
+
         def open_half(w):
             for copy in fetch_w(w):
                 copy.wait()
 
-            for copy in fetch_w(w + 1):
-                copy.start()
+            @pl.when(odd(w) == 1)
+            def _():
+                fetch_pair(w + 1)
 
         def term_of(i, m, slot, j):
             left = (h_ring, h_ring, y_ring)[i]
@@ -400,13 +403,7 @@
 
         @pl.when(w_lag < 2)
         def _():
-            for copy in fetch_w(0):
-                copy.start()
-
-        @pl.when(last)
-        def _():
-            for copy in fetch_w(1):
-                copy.start()
+            fetch_pair(0)
 
         for block in range(acc.shape[0]):
             acc[block] = jnp.zeros(acc.shape[1:], f32)
@@ -416,8 +413,7 @@
 
             @pl.when((w_lag > 1) & (j == w_lag - 1))
             def _():
-                for copy in fetch_w(0):
-                    copy.start()
+                fetch_pair(0)
 
             return 0
 
@@ -440,11 +436,6 @@
             for tile in half_tiles:
                 tile(done)
 
-        @pl.when(jnp.logical_not(last))
-        def _():
-            for copy in fetch_w(2 * half_of(done + 1) + 1):
-                copy.start()
-
         def open_whole(m):
             with jax.named_scope("wait_w"):
                 for w in (2 * m, 2 * m + 1):
@@ -453,9 +444,7 @@
 
         def whole_w(m, _):
             open_whole(m)
-            for w in (2 * m + 2, 2 * m + 3):
-                for copy in fetch_w(w):
-                    copy.start()
+            fetch_pair(2 * m + 2)
             with jax.named_scope("WW"):
                 for i, j in ((i, j) for i in range(3) for j in range(per)):
                     w_add(acc.at[i * per + j], term_of(i, m, 2 * odd(m) + j // (per // 2), j % (per // 2)))

time: 239 us -> 237 us (level)
  no operation moved by 1% of the time
where the time goes in v4:
time: 237 us; the launch traced here: 236 us
  Pallas kernels  232 us (98%)
  local copies, waits for them, and re-layouts  3.82 us (2%)
    pallas_call x1, Pallas kernels, step(): pl.pallas_call(functools.partial(kernel, stages, micro), out_shape=[out,...  232 us

profile of v4, /device:TPU:3, one launch (start us, length us, event | category | flops | bytes accessed | tf_op | source)
XLA Modules:
  0.0 236.3 jit_solution(6282634024249980324)
XLA Ops:
  0.6 231.8 %shard_map.76 = (bf16[1,640,1536]{2,1,0:T(8,128)(2,1)S(1)}, bf16[1,640,1536]{2,1,0:T(8,128)(2,1)S(1)}, bf16[1,1536,640]{2,1,0:T(8,128)(2,1)S(1)}, f32[32,1536,25...) custom-call(bf16[16,512,640]{2,1,0:T(8,128)(2,1)} %x.1, ...), custom_call_target="tpu_custom_call" | custom-call | tf_op jit(solution)/shard_map/pallas_call | solution.py:509
  232.5 1.3 copy.11
  233.7 1.3 copy.12
  235.0 1.3 copy.13

commit v5 on v4

--- a/solution.py
+++ b/solution.py
@@ -12,7 +12,7 @@
 CHUNK = 256
 SENDS = 5
 SUB = 64
-LEADS = (32, 25, 20, 17, 12, 9, 4, 1)
+LEADS = (32, 26, 20, 17, 12, 9, 4, 1)
 
 
 def dot(a, b):
@@ -371,6 +371,8 @@
                 for i, k in enumerate((k_dg, k_du, k_mid))
             ]
 
+        done = rest - w_lag
+
         def fetch_pair(w):
             for copy in fetch_w(w) + fetch_w(w + 1):
                 copy.start()
@@ -379,9 +381,15 @@
             for copy in fetch_w(w):
                 copy.wait()
 
-            @pl.when(odd(w) == 1)
-            def _():
-                fetch_pair(w + 1)
+            @pl.when(w < done)
+            def _():
+                for copy in fetch_w(w + 1):
+                    copy.start()
+
+            @pl.when(w >= done - 1)
+            def _():
+                for copy in fetch_w(w + 2):
+                    copy.start()
 
         def term_of(i, m, slot, j):
             left = (h_ring, h_ring, y_ring)[i]
@@ -403,7 +411,13 @@
 
         @pl.when(w_lag < 2)
         def _():
-            fetch_pair(0)
+            for copy in fetch_w(0):
+                copy.start()
+
+        @pl.when(last)
+        def _():
+            for copy in fetch_w(1):
+                copy.start()
 
         for block in range(acc.shape[0]):
             acc[block] = jnp.zeros(acc.shape[1:], f32)
@@ -413,7 +427,8 @@
 
             @pl.when((w_lag > 1) & (j == w_lag - 1))
             def _():
-                fetch_pair(0)
+                for copy in fetch_w(0):
+                    copy.start()
 
             return 0
 
@@ -427,8 +442,6 @@
         for c in (n - 2, n - 1):
             for copy in keep_d(c):
                 copy.wait()
-
-        done = rest - w_lag
 
         @pl.when(odd(done) == 1)
         def _():

time: 237 us -> 235 us (level)
  no operation moved by 1% of the time
where the time goes in v5:
time: 235 us; the launch traced here: 234 us
  Pallas kernels  230 us (98%)
  local copies, waits for them, and re-layouts  3.82 us (2%)
    pallas_call x1, Pallas kernels, step(): pl.pallas_call(functools.partial(kernel, stages, micro), out_shape=[out,...  230 us

profile of v5, /device:TPU:3, one launch (start us, length us, event | category | flops | bytes accessed | tf_op | source)
XLA Modules:
  0.0 234.3 jit_solution(2427614149235196950)
XLA Ops:
  0.6 229.9 %shard_map.76 = (bf16[1,640,1536]{2,1,0:T(8,128)(2,1)S(1)}, bf16[1,640,1536]{2,1,0:T(8,128)(2,1)S(1)}, bf16[1,1536,640]{2,1,0:T(8,128)(2,1)S(1)}, f32[32,1536,25...) custom-call(bf16[16,512,640]{2,1,0:T(8,128)(2,1)} %x.1, ...), custom_call_target="tpu_custom_call" | custom-call | tf_op jit(solution)/shard_map/pallas_call | solution.py:522
  230.5 1.3 copy.11
  231.8 1.3 copy.12
  233.1 1.3 copy.13
